TPU v7x, 32 devices: a whole 2x2x4 slice. The times are simulated.
32 devices in a mesh: frames: 8 (over z, x), rows: 4 (over y, core).
Axes of the slice: x: 2, y: 2, z: 4, core: 2. Of those that a mesh axis runs over, the one named last changes fastest.
Arguments:
- fmap: bfloat16 [16, 12, 64, 128], P('frames', 'rows'), may hold values from -6 to 6
- context: bfloat16 [16, 12, 64, 128], P('frames', 'rows'), may hold values from -6 to 6
- pairs: int32 [32, 3], replicated, may hold values from 0 to 15, as said below
- w_corr: bfloat16 [49, 128], replicated, may hold values from -0.875 to 0.875
- w_zr: bfloat16 [256, 256], replicated, may hold values from -0.375 to 0.375
- w_q: bfloat16 [9, 256, 128], replicated, may hold values from -0.125 to 0.125
- w_msg: bfloat16 [128, 256], replicated, may hold values from -0.5 to 0.5
- w_res: bfloat16 [9, 128, 128], replicated, may hold values from -0.1875 to 0.1875
Outputs:
- state: bfloat16 [16, 12, 64, 128], P('frames', 'rows')
Inputs may be any that keep to these rules, and one draw needn't show every extreme that they name: Source and target differ. With dev(f) = f // 2, the source's dev, the target's dev and the owner differ pairwise by at most one. No owner holds more than 8 pairs, and some owner holds exactly 8.
All inputs are finite; a program needn't handle non-finite values.
Results may differ from a plain program's by a relative error of at most 0.01.
Values may be sent and summed in bfloat16 or wider, within the bound.
A program may use at most 64 MiB of HBM per device.

v0:
```python
import functools

import jax
import jax.numpy as jnp
from jax import lax
from jax.experimental import pallas as pl
from jax.experimental.pallas import tpu as pltpu
from jax.sharding import PartitionSpec as P

RADIUS = 3
ROUNDS = 2
CAPACITY = 8
LANES = 128
MESH = pl.DeviceIdType.MESH
F32 = jnp.float32
BF16 = jnp.bfloat16
LEFT, RIGHT, UP, DOWN = range(4)


def dot(a, b):
    return jnp.dot(a, b, preferred_element_type=F32)


def dot_nt(a, b):
    return lax.dot_general(a, b, (((1,), (1,)), ((), ())), preferred_element_type=F32)


def kernel(
    nf, nr,
    pairs_ref, fmap_ref, ctx_ref, wcorr_ref, wzr_ref, wq_ref, wmsg_ref, wres_ref,
    out_ref,
    fwin, cwin, motion, hid, zbuf, qr, qx, msend, mrecv, mown, ubuf, sbuf,
    wsel, wq_s, wres_s, wmsg_s, pre, rim, tbl,
    ssem, rsem, lsem,
):
    f = lax.axis_index("frames")
    r = lax.axis_index("rows")
    fd, height, width, chans = fmap_ref.shape
    npair = pairs_ref.shape[0]
    rows = height * width
    has = {LEFT: f > 0, RIGHT: f < nf - 1, UP: r > 0, DOWN: r < nr - 1}
    dev = {LEFT: (f - 1, r), RIGHT: (f + 1, r), UP: (f, r - 1), DOWN: (f, r + 1)}
    back = {LEFT: RIGHT, RIGHT: LEFT, UP: DOWN, DOWN: UP}
    sent = []

    def both(cond, gate):
        return cond if gate is None else jnp.logical_and(cond, gate)

    def rcopy(handle):
        i, way, src, dst, _ = handle
        return pltpu.make_async_remote_copy(
            src_ref=src, dst_ref=dst, send_sem=ssem.at[i], recv_sem=rsem.at[i],
            device_id=dev[way], device_id_type=MESH,
        )

    def push(way, src, dst, gate=None):
        handle = (len(sent), way, src, dst, gate)
        sent.append(handle)

        @pl.when(both(has[way], gate))
        def _():
            rcopy(handle).start()

        return handle

    def arrive(handle):
        @pl.when(both(has[back[handle[1]]], handle[4]))
        def _():
            rcopy(handle).wait_recv()

    own_rows = pl.ds(RADIUS, height)
    place = {RIGHT: pl.ds(0, fd), LEFT: pl.ds(2 * fd, fd)}
    middle = pl.ds(fd, fd)

    own_f = pltpu.make_async_copy(fmap_ref, fwin.at[middle, own_rows], lsem.at[0])
    own_c = pltpu.make_async_copy(ctx_ref, cwin.at[0, middle], lsem.at[1])
    loads = []
    for k in range(3):
        for j in range(3):
            lanes = pl.ds(j * chans, chans)
            loads.append((wq_ref.at[3 * k + j], wq_s.at[k, :, lanes]))
            loads.append((wres_ref.at[3 * k + j], wres_s.at[k, :, lanes]))
    loads = [
        pltpu.make_async_copy(src, dst, lsem.at[2 + n]) for n, (src, dst) in enumerate(loads)
    ]

    barrier = pltpu.get_barrier_semaphore()
    count = 0
    for way in (LEFT, RIGHT, UP, DOWN):
        count = count + has[way].astype(jnp.int32)

        @pl.when(has[way])
        def _(way=way):
            pl.semaphore_signal(barrier, inc=1, device_id=dev[way], device_id_type=MESH)

    own_f.start()
    own_c.start()
    for load in loads:
        load.start()
    pl.semaphore_wait(barrier, count)

    seat = {RIGHT: 0, LEFT: 2 * fd}
    feats = {}
    for j in range(fd):
        for way in (RIGHT, LEFT):
            feats[way, j] = push(way, fmap_ref.at[j], fwin.at[seat[way] + j, own_rows])
    edge_src = {UP: pl.ds(RADIUS, RADIUS), DOWN: pl.ds(height, RADIUS)}
    edge_dst = {UP: pl.ds(RADIUS + height, RADIUS), DOWN: pl.ds(0, RADIUS)}
    feat_edge = {UP: pl.ds(0, RADIUS), DOWN: pl.ds(height - RADIUS, RADIUS)}
    edges = [
        push(way, fmap_ref.at[:, feat_edge[way]], fwin.at[middle, edge_dst[way]])
        for way in (UP, DOWN)
    ]
    states = [push(way, ctx_ref, cwin.at[0, place[way]]) for way in (RIGHT, LEFT)]

    fwin[:, 2 * RADIUS + height] = jnp.zeros(
        (fwin.shape[0],) + fwin.shape[2:], BF16
    )

    @pl.when(r == 0)
    def _():
        fwin[:, 0:RADIUS] = jnp.zeros((fwin.shape[0], RADIUS, width, chans), BF16)
        for k in range(ROUNDS):
            qr[k, :, 0] = jnp.zeros((CAPACITY, width, chans), BF16)
            qx[k, :, 0] = jnp.zeros((CAPACITY, width, chans), BF16)
            ubuf[k, :, 0] = jnp.zeros((fd, width, chans), BF16)

    @pl.when(r == nr - 1)
    def _():
        fwin[:, RADIUS + height : 2 * RADIUS + height] = jnp.zeros(
            (fwin.shape[0], RADIUS, width, chans), BF16
        )
        for k in range(ROUNDS):
            qr[k, :, height + 1] = jnp.zeros((CAPACITY, width, chans), BF16)
            qx[k, :, height + 1] = jnp.zeros((CAPACITY, width, chans), BF16)
            ubuf[k, :, height + 1] = jnp.zeros((fd, width, chans), BF16)

    for way, edge in ((RIGHT, f == 0), (LEFT, f == nf - 1)):
        @pl.when(edge)
        def _(way=way):
            fwin[place[way]] = jnp.zeros((fd,) + fwin.shape[1:], BF16)
            for k in range(ROUNDS):
                cwin[k, place[way]] = jnp.zeros((fd, height, width, chans), BF16)
                mrecv[k, way] = jnp.zeros((fd, rows, chans), BF16)

    zero = jnp.int32(0)

    def pick(p, carry):
        seen, srcs, tgts, ok = carry
        mine = (pairs_ref[p, 2] == f).astype(jnp.int32)
        s, t = pairs_ref[p, 0], pairs_ref[p, 1]
        hits = [mine * (seen == k).astype(jnp.int32) for k in range(CAPACITY)]
        srcs = tuple(v + h * s for v, h in zip(srcs, hits))
        tgts = tuple(v + h * t for v, h in zip(tgts, hits))
        ok = tuple(v + h for v, h in zip(ok, hits))
        return seen + mine, srcs, tgts, ok

    zeros = (zero,) * CAPACITY
    _, srcs, tgts, oks = lax.fori_loop(0, npair, pick, (zero, zeros, zeros, zeros))
    first = (f - 1) * fd
    last = 3 * fd - 1
    for k in range(CAPACITY):
        s_idx = jnp.clip(srcs[k] - first, 0, last)
        t_idx = jnp.clip(tgts[k] - first, 0, last)
        tbl[0, k] = s_idx
        tbl[1, k] = t_idx
        tbl[2, k] = jnp.where(oks[k] == 1, s_idx, -1)
        tbl[3, k] = jnp.where(oks[k] == 1, t_idx, -1)

    span = 2 * RADIUS + 1
    per = LANES // width
    groups = (span + per - 1) // per
    depth = groups * LANES
    line = lax.broadcasted_iota(jnp.int32, (depth, wcorr_ref.shape[0]), 0)
    col = lax.broadcasted_iota(jnp.int32, (depth, wcorr_ref.shape[0]), 1)
    lane = lax.rem(line, LANES) + RADIUS + 1
    b_off = lax.rem(lane, width)
    a_off = lax.div(line, LANES) * per + lax.rem(lax.div(lane, width) + per - 1, per)
    take = jnp.logical_and(b_off < span, a_off < span)
    index = jnp.where(take, a_off * span + b_off, -1)
    wsel[...] = dot(
        jnp.where(index == col, 1.0, 0.0).astype(BF16), wcorr_ref[...]
    ).astype(BF16)
    wmsg_s[0:chans] = wmsg_ref[:, 0:chans]
    wmsg_s[chans : 2 * chans] = wmsg_ref[:, chans : 2 * chans]

    own_f.wait()
    for j in range(fd):
        for way in (RIGHT, LEFT):
            arrive(feats[way, j])
            spot = seat[way] + j
            for side in (UP, DOWN):
                edges.append(
                    push(
                        side, fwin.at[spot, edge_src[side]], fwin.at[spot, edge_dst[side]],
                        gate=has[back[way]],
                    )
                )
    for handle in edges:
        arrive(handle)

    xs = width - 1 - lax.broadcasted_iota(jnp.int32, (width, LANES), 0)
    ls = lax.broadcasted_iota(jnp.int32, (width, LANES), 1) + RADIUS + 1
    bs = lax.rem(ls, width)
    flip = jnp.where(
        lax.broadcasted_iota(jnp.int32, (width, width), 0)
        + lax.broadcasted_iota(jnp.int32, (width, width), 1)
        == width - 1,
        1.0,
        0.0,
    ).astype(BF16)
    inside = jnp.logical_and(xs + bs >= RADIUS, xs + bs < width + RADIUS)
    inside = jnp.logical_and(inside, bs < span)
    scale = 1.0 / chans**0.5

    @pl.loop(0, CAPACITY, unroll=4)
    def _(s):
        src_i, tgt_i = tbl[0, s], tbl[1, s]
        lines = []
        for y in range(height):
            a = dot(flip, fwin[src_i, RADIUS + y]).astype(BF16)
            b = fwin[tgt_i, pl.ds(y, groups * per)].reshape(groups * per * width, chans)
            g = dot_nt(a, b) * scale
            tiles = []
            for j in range(groups):
                tile = pltpu.roll(
                    g[:, j * LANES : (j + 1) * LANES], 0, 1, stride=1, stride_axis=0
                )
                tiles.append(jnp.where(inside, tile, 0.0).astype(BF16))
            lines.append(jnp.concatenate(tiles, axis=1))
        corr = jnp.concatenate(lines, axis=0)
        moved = jnp.maximum(dot(corr, wsel[...]), 0.0).astype(BF16)
        for y in range(height):
            motion[s, y * width : (y + 1) * width] = dot(
                flip, moved[y * width : (y + 1) * width]
            ).astype(BF16)

    own_c.wait()
    for load in loads:
        load.wait()

    def shifted_sum(acc):
        rows = acc.shape[0]
        line_no = lax.rem(lax.broadcasted_iota(jnp.int32, (rows, chans), 0), width)
        not_first = line_no > 0
        not_last = line_no < width - 1
        before = pltpu.roll(acc[:, 0:chans], 1, 0)
        after = pltpu.roll(acc[:, 2 * chans : 3 * chans], rows - 1, 0)
        return (
            jnp.where(not_first, before, 0.0)
            + acc[:, chans : 2 * chans]
            + jnp.where(not_last, after, 0.0)
        )

    def conv_own(part, weight):
        blank = jnp.zeros((width, 3 * chans), F32)
        acc = dot(part, weight[1])
        if height > 1:
            acc = acc + jnp.concatenate([blank, dot(part[: rows - width], weight[0])], axis=0)
            acc = acc + jnp.concatenate([dot(part[width:], weight[2]), blank], axis=0)
        return shifted_sum(acc)

    halo_src = {UP: 1, DOWN: height}
    halo_dst = {UP: height + 1, DOWN: 0}

    for k in range(ROUNDS):
        for handle in states:
            arrive(handle)

        @pl.loop(0, CAPACITY, unroll=4)
        def _(s):
            state = cwin[k, tbl[0, s]].reshape(rows, chans).astype(F32)
            if k == 0:
                hid[s] = jnp.tanh(state)
            xin = (motion[s].astype(F32) + state).astype(BF16)
            qx[k, s, pl.ds(1, height)] = xin.reshape(height, width, chans)

        halos = [
            push(side, qx.at[k, :, halo_src[side]], qx.at[k, :, halo_dst[side]])
            for side in (UP, DOWN)
        ]

        @pl.loop(0, CAPACITY, unroll=4)
        def _(s):
            h = hid[s]
            xin = qx[k, s, pl.ds(1, height)].reshape(rows, chans)
            gates = jax.nn.sigmoid(dot(jnp.concatenate([h.astype(BF16), xin], axis=1), wzr_ref[...]))
            zbuf[s] = gates[:, 0:chans]
            qr[k, s, pl.ds(1, height)] = (
                (gates[:, chans : 2 * chans] * h).astype(BF16).reshape(height, width, chans)
            )

        halos += [
            push(side, qr.at[k, :, halo_src[side]], qr.at[k, :, halo_dst[side]])
            for side in (UP, DOWN)
        ]

        @pl.loop(0, CAPACITY, unroll=4)
        def _(s):
            part = jnp.concatenate(
                [
                    qr[k, s, pl.ds(1, height)].reshape(rows, chans),
                    qx[k, s, pl.ds(1, height)].reshape(rows, chans),
                ],
                axis=1,
            )
            pre[s] = conv_own(part, wq_s)

        for handle in halos:
            arrive(handle)
        for n, (line_at, tap) in enumerate(((0, 0), (height + 1, 2))):
            part = jnp.concatenate(
                [
                    qr[k, :, line_at].reshape(CAPACITY * width, chans),
                    qx[k, :, line_at].reshape(CAPACITY * width, chans),
                ],
                axis=1,
            )
            rim[n] = shifted_sum(dot(part, wq_s[tap])).reshape(CAPACITY, width, chans)

        @pl.loop(0, CAPACITY, unroll=4)
        def _(s):
            for y in range(height):
                piece = pl.ds(y * width, width)
                total = pre[s, piece]
                if y == 0:
                    total = total + rim[0, s]
                if y == height - 1:
                    total = total + rim[1, s]
                z = zbuf[s, piece]
                hid[s, piece] = (1.0 - z) * hid[s, piece] + z * jnp.tanh(total)

        def message(j):
            first_sum = jnp.zeros((rows, chans), F32)
            second_sum = jnp.zeros((rows, chans), F32)
            for s in range(CAPACITY):
                h = hid[s]
                first_sum = first_sum + jnp.where(tbl[2, s] == j, 1.0, 0.0) * h
                second_sum = second_sum + jnp.where(tbl[3, s] == j, 1.0, 0.0) * h
            both = jnp.concatenate([first_sum.astype(BF16), second_sum.astype(BF16)], axis=1)
            return dot(both, wmsg_s[...])

        parcels = []
        for j in range(fd):
            for way, start in ((LEFT, 0), (RIGHT, 2 * fd)):
                msend[k, way, j] = message(start + j).astype(BF16)
                parcels.append(push(way, msend.at[k, way, j], mrecv.at[k, way, j]))
        for j in range(fd):
            mown[j] = message(fd + j)
        for handle in parcels:
            arrive(handle)
        for j in range(fd):
            total = mown[j] + mrecv[k, LEFT, j].astype(F32) + mrecv[k, RIGHT, j].astype(F32)
            ubuf[k, j, pl.ds(1, height)] = (
                jnp.maximum(total, 0.0).astype(BF16).reshape(height, width, chans)
            )
        halos = [
            push(side, ubuf.at[k, :, halo_src[side]], ubuf.at[k, :, halo_dst[side]])
            for side in (UP, DOWN)
        ]
        for j in range(fd):
            part = ubuf[k, j, pl.ds(1, height)].reshape(rows, chans)
            mown[j] = cwin[k, fd + j].reshape(rows, chans).astype(F32) + conv_own(part, wres_s)
        for handle in halos:
            arrive(handle)
        states = []
        for j in range(fd):
            top = shifted_sum(dot(ubuf[k, j, 0], wres_s[0]))
            bottom = shifted_sum(dot(ubuf[k, j, height + 1], wres_s[2]))
            for y in range(height):
                total = mown[j, y * width : (y + 1) * width]
                if y == 0:
                    total = total + top
                if y == height - 1:
                    total = total + bottom
                if k == ROUNDS - 1:
                    out_ref[j, y] = total.astype(BF16)
                else:
                    sbuf[k, j, y] = total.astype(BF16)
                    cwin[k + 1, fd + j, y] = total.astype(BF16)
            if k < ROUNDS - 1:
                for way in (RIGHT, LEFT):
                    states.append(push(way, sbuf.at[k, j], cwin.at[k + 1, seat[way] + j]))

    for handle in sent:
        @pl.when(both(has[handle[1]], handle[4]))
        def _(handle=handle):
            rcopy(handle).wait_send()


def local(nf, nr, fmap, context, pairs, w_corr, w_zr, w_q, w_msg, w_res):
    fd, height, width, chans = fmap.shape
    rows = height * width
    win = 3 * fd
    groups = -(-(2 * RADIUS + 1) // (LANES // width))
    copies = 6 * fd + 4 + ROUNDS * (6 + 2 * fd) + (ROUNDS - 1) * 2 * fd
    vmem = pl.BlockSpec(memory_space=pltpu.VMEM)
    hbm = pl.BlockSpec(memory_space=pl.ANY)
    return pl.pallas_call(
        functools.partial(kernel, nf, nr),
        out_shape=jax.ShapeDtypeStruct(fmap.shape, BF16),
        in_specs=[
            pl.BlockSpec(memory_space=pltpu.SMEM), vmem, vmem, vmem, vmem, hbm, vmem, hbm,
        ],
        out_specs=vmem,
        scratch_shapes=[
            pltpu.VMEM((win, 2 * RADIUS + height + 1, width, chans), BF16),
            pltpu.VMEM((ROUNDS, win, height, width, chans), BF16),
            pltpu.VMEM((CAPACITY, rows, chans), BF16),
            pltpu.VMEM((CAPACITY, rows, chans), F32),
            pltpu.VMEM((CAPACITY, rows, chans), F32),
            pltpu.VMEM((ROUNDS, CAPACITY, height + 2, width, chans), BF16),
            pltpu.VMEM((ROUNDS, CAPACITY, height + 2, width, chans), BF16),
            pltpu.VMEM((ROUNDS, 2, fd, rows, chans), BF16),
            pltpu.VMEM((ROUNDS, 2, fd, rows, chans), BF16),
            pltpu.VMEM((fd, rows, chans), F32),
            pltpu.VMEM((ROUNDS, fd, height + 2, width, chans), BF16),
            pltpu.VMEM((ROUNDS, fd, height, width, chans), BF16),
            pltpu.VMEM((groups * LANES, chans), BF16),
            pltpu.VMEM((3, 2 * chans, 3 * chans), BF16),
            pltpu.VMEM((3, chans, 3 * chans), BF16),
            pltpu.VMEM((2 * chans, chans), BF16),
            pltpu.VMEM((CAPACITY, rows, chans), F32),
            pltpu.VMEM((2, CAPACITY, width, chans), F32),
            pltpu.SMEM((4, CAPACITY), jnp.int32),
            pltpu.SemaphoreType.DMA((copies,)),
            pltpu.SemaphoreType.DMA((copies,)),
            pltpu.SemaphoreType.DMA((20,)),
        ],
        compiler_params=pltpu.CompilerParams(collective_id=0, has_side_effects=True),
    )(pairs, fmap, context, w_corr, w_zr, w_q, w_msg, w_res)


def solution(mesh):
    placed = (P("frames", "rows", None, None), P("frames", "rows", None, None)) + (P(),) * 6
    return jax.shard_map(
        functools.partial(local, mesh.shape["frames"], mesh.shape["rows"]),
        mesh=mesh,
        in_specs=placed,
        out_specs=P("frames", "rows", None, None),
        check_vma=False,
    )
```

profile of v0, /device:TPU:9, one launch (start us, length us, event | category | flops | bytes accessed | tf_op | source)
XLA Modules:
  0.0 56.4 jit_solution(12639979147344346604)
XLA Ops:
  0.0 1.4 %copy.9.pairs_ref = s32[32,3]{1,0:T(8,128)} copy(s32[32,3]{0,1:T(4,128)} %param.10) | data formatting | bytes 768 | tf_op args[2]
  1.4 53.5 %shard_map.82 = bf16[2,3,64,128]{3,2,1,0:T(8,128)(2,1)} custom-call(s32[32,3]{1,0:T(8,128)} %copy.9.pairs_ref, bf16[2,3,64,128]{3,2,1,0:T(8,128)(2,1)} %fmap_ref.1, bf16[2,3,64,128]{3,2,1,0:T(8,128)(2,1)} %ctx_ref.1, bf16[49,128]{1,0:T(8,128)(2,1)} %wcorr_ref.1, bf16[256,256]{1,0:T(8,128)(2,1)} %wzr_ref.1, bf16[9,256,128]{2,1,0:T(8,128)(2,1)} %wq_ref.1, ...), custom_call_target="tpu_custom_call" | custom-call | tf_op jit(solution)/shard_map/pallas_call | solution.py:399
  54.8 1.5 %copy.11 = bf16[2,3,64,128]{3,2,1,0:T(8,128)(2,1)} copy(bf16[2,3,64,128]{3,2,1,0:T(8,128)(2,1)} %shard_map.82) | data formatting | bytes 196608
where the time goes:
time: 56.6 us; the launch traced here: 56.4 us
  Pallas kernels  53.5 us (95%)
  local copies, waits for them, and re-layouts  2.91 us (5%)
    pallas_call x1, Pallas kernels, local(): pl.pallas_call(functools.partial(kernel, nf, nr), out_shape=jax.ShapeDtyp...  53.5 us
    unnamed x2, local copies, waits for them, and re-layouts  2.91 us

commit v1 on v0

v1 whole, which is shorter than its diff:
```python
import functools

import jax
import jax.numpy as jnp
from jax import lax
from jax.experimental import pallas as pl
from jax.experimental.pallas import tpu as pltpu
from jax.sharding import PartitionSpec as P

RADIUS = 3
ROUNDS = 2
LANES = 128
SPAN = 2 * RADIUS + 1
MESH = pl.DeviceIdType.MESH
F32 = jnp.float32
BF16 = jnp.bfloat16
LEFT, RIGHT, UP, DOWN = range(4)


def dot(a, b):
    return jnp.dot(a, b, preferred_element_type=F32)


def dot_nt(a, b):
    return lax.dot_general(a, b, (((1,), (1,)), ((), ())), preferred_element_type=F32)


def plan(fd):
    groups = []
    for j in range(fd):
        for way, seat in ((LEFT, j), (RIGHT, 2 * fd + j)):
            groups.append((way, j, [(i, seat) for i in range(fd)]))
    groups.append((None, 0, [(i, fd + j) for j in range(fd) for i in range(fd) if i != j]))
    start = 0
    out = []
    for way, j, members in groups:
        out.append((way, j, start, members))
        start += len(members)
    return out, start


def kernel(
    nf, nr,
    pairs_ref, fmap_ref, ctx_ref, wcorr_ref, wzr_ref, wq_ref, wmsg_ref, wres_ref,
    out_ref,
    fsrc, fwin, st, mot, hid, hh, th, hw0, hw, qbuf, zbuf, asum, bsum,
    msend, mrecv, ubuf, mown,
    wcorr_s, wsel, wzr_s, wq_s, wres_s, wmsg_s, tbl,
    ssem, rsem, lsem,
):
    f = lax.axis_index("frames")
    r = lax.axis_index("rows")
    height, fd, width, chans = fsrc.shape
    npair = pairs_ref.shape[1]
    rows = height * width
    tall = (height + 2) * width
    groups, total_combos = plan(fd)
    has = {LEFT: f > 0, RIGHT: f < nf - 1, UP: r > 0, DOWN: r < nr - 1}
    dev = {LEFT: (f - 1, r), RIGHT: (f + 1, r), UP: (f, r - 1), DOWN: (f, r + 1)}
    back = {LEFT: RIGHT, RIGHT: LEFT, UP: DOWN, DOWN: UP}
    sent = []

    def both(cond, gate):
        return cond if gate is None else jnp.logical_and(cond, gate)

    def rcopy(handle):
        i, way, src, dst, _ = handle
        return pltpu.make_async_remote_copy(
            src_ref=src, dst_ref=dst, send_sem=ssem.at[i], recv_sem=rsem.at[i],
            device_id=dev[way], device_id_type=MESH,
        )

    def push(way, src, dst, gate=None):
        handle = (len(sent), way, src, dst, gate)
        sent.append(handle)

        @pl.when(both(has[way], gate))
        def _():
            rcopy(handle).start()

        return handle

    def arrive(handle):
        @pl.when(both(has[back[handle[1]]], handle[4]))
        def _():
            rcopy(handle).wait_recv()

    own_rows = pl.ds(RADIUS, height)
    middle = pl.ds(fd, fd)
    seat = {RIGHT: 0, LEFT: 2 * fd}

    barrier = pltpu.get_barrier_semaphore()
    count = 0
    for way in (LEFT, RIGHT, UP, DOWN):
        count = count + has[way].astype(jnp.int32)

        @pl.when(has[way])
        def _(way=way):
            pl.semaphore_signal(barrier, inc=1, device_id=dev[way], device_id_type=MESH)

    loads = []

    def load(src, dst):
        copy = pltpu.make_async_copy(src, dst, lsem.at[len(loads)])
        loads.append(copy)
        copy.start()
        return copy

    own_f = [load(fmap_ref.at[i], fsrc.at[:, i]) for i in range(fd)]
    own_c = load(ctx_ref, st.at[0, :, pl.ds(1, height)])
    corr_w = load(wcorr_ref, wcorr_s)
    gate_w = load(wzr_ref, wzr_s)
    late = []
    for k in range(3):
        for j in range(3):
            lanes = pl.ds(j * chans, chans)
            late.append(load(wq_ref.at[3 * k + j], wq_s.at[pl.ds(2 * k * chans, 2 * chans), lanes]))
            late.append(load(wres_ref.at[3 * k + j], wres_s.at[pl.ds(k * chans, chans), lanes]))
    for k in range(2):
        lanes = pl.ds(k * chans, chans)
        late.append(load(wmsg_ref.at[:, lanes], wmsg_s.at[lanes]))

    flip = jnp.where(
        lax.broadcasted_iota(jnp.int32, (width, width), 0)
        + lax.broadcasted_iota(jnp.int32, (width, width), 1)
        == width - 1,
        1.0,
        0.0,
    ).astype(BF16)
    for copy in own_f:
        copy.wait()
    for i in range(fd):
        for y in range(height):
            fwin[fd + i, RADIUS + y] = dot(flip, fsrc[y, i]).astype(BF16)
    pl.semaphore_wait(barrier, count)

    feats = {}
    edge_src = {UP: pl.ds(RADIUS, RADIUS), DOWN: pl.ds(height, RADIUS)}
    edge_dst = {UP: pl.ds(RADIUS + height, RADIUS), DOWN: pl.ds(0, RADIUS)}
    own_edges = []
    for j in range(fd):
        for way in (RIGHT, LEFT):
            feats[way, j] = push(
                way, fwin.at[fd + j, own_rows], fwin.at[seat[way] + j, own_rows]
            )
        if j == 0:
            own_edges = [
                push(way, fwin.at[middle, edge_src[way]], fwin.at[middle, edge_dst[way]])
                for way in (UP, DOWN)
            ]
    line_src = {UP: 1, DOWN: height}
    line_dst = {UP: height + 1, DOWN: 0}
    own_c.wait()
    ctx_edges = [
        push(way, st.at[0, :, line_src[way]], st.at[0, :, line_dst[way]]) for way in (UP, DOWN)
    ]

    fwin[:, 2 * RADIUS + height] = jnp.zeros((fwin.shape[0],) + fwin.shape[2:], BF16)
    for way, edge in ((UP, r == 0), (DOWN, r == nr - 1)):
        @pl.when(edge)
        def _(way=way):
            outside = back[way]
            fwin[:, edge_dst[outside]] = jnp.zeros(
                (fwin.shape[0], RADIUS, width, chans), BF16
            )
            line = line_dst[outside]
            mot[:, line] = jnp.zeros((total_combos, width, chans), BF16)
            hh[:, :, line] = jnp.zeros(hh.shape[:2] + (width, chans), BF16)
            st[0, :, line] = jnp.zeros((fd, width, chans), BF16)
            first = 0 if way == UP else height + 2
            ubuf[:, :, first : first + 2] = jnp.zeros((ROUNDS, fd, 2, width, chans), BF16)

    for way, edge in ((RIGHT, f == 0), (LEFT, f == nf - 1)):
        @pl.when(edge)
        def _(way=way):
            fwin[seat[way] : seat[way] + fd] = jnp.zeros((fd,) + fwin.shape[1:], BF16)
            for k in range(ROUNDS):
                mrecv[k, way] = jnp.zeros((fd, rows, chans), BF16)

    window = 3 * fd
    base_s = f * fd
    base_t = (f - 1) * fd
    codes = [i * window + j for _, _, _, members in groups for i, j in members]

    def tally(p, counts):
        i = pairs_ref[0, p] - base_s
        j = pairs_ref[1, p] - base_t
        own = jnp.logical_and(i >= 0, i < fd)
        code = jnp.where(own, i * window + j, -1)
        return tuple(v + (code == c).astype(jnp.int32) for v, c in zip(counts, codes))

    counts = lax.fori_loop(0, npair, tally, (jnp.int32(0),) * total_combos)
    for c in range(total_combos):
        tbl[c] = counts[c]

    def times(c):
        return tbl[c].astype(F32)

    per = LANES // width
    tiles = (SPAN + per - 1) // per
    depth = tiles * LANES
    origin = width - 1 - RADIUS

    def place(lane):
        spot = lax.rem(lane + (LANES - origin), LANES)
        return lax.div(spot, width), (SPAN - 1) - lax.rem(spot, width)

    corr_w.wait()
    line = lax.broadcasted_iota(jnp.int32, (depth, wcorr_s.shape[0]), 0)
    col = lax.broadcasted_iota(jnp.int32, (depth, wcorr_s.shape[0]), 1)
    half, b_off = place(lax.rem(line, LANES))
    a_off = lax.div(line, LANES) * per + half
    take = jnp.logical_and(b_off >= 0, a_off < SPAN)
    index = jnp.where(take, a_off * SPAN + b_off, -1)
    wsel[...] = dot(jnp.where(index == col, 1.0, 0.0).astype(BF16), wcorr_s[...]).astype(BF16)

    xs = lax.broadcasted_iota(jnp.int32, (width, LANES), 0)
    _, bs = place(lax.broadcasted_iota(jnp.int32, (width, LANES), 1))
    inside = jnp.logical_and(xs + bs >= RADIUS, xs + bs < width + RADIUS)
    inside = jnp.logical_and(inside, bs >= 0)
    scale = 1.0 / chans**0.5

    def banded(g):
        pieces = []
        for q in range(tiles):
            piece = pltpu.roll(g[:, q * LANES : (q + 1) * LANES], 0, 1, stride=1, stride_axis=0)
            pieces.append(jnp.where(inside, piece, 0.0).astype(BF16))
        return jnp.concatenate(pieces, axis=1)

    def correlate(group):
        way, _, start, members = group
        lines = [[] for _ in members]
        for y in range(height):
            if way is None:
                for n, (i, j) in enumerate(members):
                    b = fwin[j, y : y + tiles * per].reshape(tiles * per * width, chans)
                    lines[n].append(banded(dot_nt(fsrc[y, i], b)))
            else:
                j = members[0][1]
                b = fwin[j, y : y + tiles * per].reshape(tiles * per * width, chans)
                g = dot_nt(fsrc[y].reshape(fd * width, chans), b)
                for n in range(fd):
                    lines[n].append(banded(g[n * width : (n + 1) * width]))
        corr = jnp.concatenate([part for each in lines for part in each], axis=0)
        moved = jnp.maximum(dot(corr, wsel[...]) * scale, 0.0).astype(BF16)
        n = len(members)
        mot[start : start + n, 1 : height + 1] = moved.reshape(n, height, width, chans)
        span = pl.ds(start, n)
        return [
            push(side, mot.at[span, line_src[side]], mot.at[span, line_dst[side]])
            for side in (UP, DOWN)
        ]

    for handle in own_edges:
        arrive(handle)
    mot_edges = {len(groups) - 1: correlate(groups[-1])}
    relays = {}
    for j in range(fd):
        for way in (RIGHT, LEFT):
            arrive(feats[way, j])
            spot = seat[way] + j
            relays[spot] = [
                push(
                    side, fwin.at[spot, edge_src[side]], fwin.at[spot, edge_dst[side]],
                    gate=has[back[way]],
                )
                for side in (UP, DOWN)
            ]
    for handle in ctx_edges:
        arrive(handle)
    gate_w.wait()
    for i in range(fd):
        first = jnp.tanh(st[0, i].reshape(tall, chans).astype(F32))
        th[i] = first
        hw0[i] = dot(first.astype(BF16), wzr_s[0:chans])
    for n, group in enumerate(groups[:-1]):
        for handle in relays[group[3][0][1]]:
            arrive(handle)
        mot_edges[n] = correlate(group)
    for copy in late:
        copy.wait()

    def shifted_sum(acc):
        line_no = lax.rem(
            lax.broadcasted_iota(jnp.int32, (acc.shape[0], chans), 0), width
        )
        before = pltpu.roll(acc[:, 0:chans], 1, 0)
        after = pltpu.roll(acc[:, 2 * chans : 3 * chans], acc.shape[0] - 1, 0)
        return (
            jnp.where(line_no > 0, before, 0.0)
            + acc[:, chans : 2 * chans]
            + jnp.where(line_no < width - 1, after, 0.0)
        )

    def recur(k, group):
        _, _, start, members = group
        n = len(members)
        for m, (i, _) in enumerate(members):
            c = start + m
            state = st[k, i].reshape(tall, chans).astype(F32)
            xin = (mot[c].reshape(tall, chans).astype(F32) + state).astype(BF16)
            known = hw0[i] if k == 0 else hw[c]
            gates = dot(xin, wzr_s[chans : 2 * chans]) + known
            zbuf[c] = jax.nn.sigmoid(gates[width : width + rows, 0:chans])
            reset = jax.nn.sigmoid(gates[:, chans : 2 * chans])
            if k == 0:
                h = th[i]
            else:
                h = jnp.concatenate(
                    [
                        hh[k - 1, c, 0].astype(F32), hid[c],
                        hh[k - 1, c, height + 1].astype(F32),
                    ],
                    axis=0,
                )
            qbuf[c, :, :, 0:chans] = (reset * h).astype(BF16).reshape(height + 2, width, chans)
            qbuf[c, :, :, chans : 2 * chans] = xin.reshape(height + 2, width, chans)
        taps = [
            qbuf[start : start + n, t : t + height].reshape(n * rows, 2 * chans) for t in range(3)
        ]
        total = shifted_sum(dot(jnp.concatenate(taps, axis=1), wq_s[...]))
        for m, (i, j) in enumerate(members):
            c = start + m
            h = th[i, width : width + rows] if k == 0 else hid[c]
            z = zbuf[c]
            h = (1.0 - z) * h + z * jnp.tanh(total[m * rows : (m + 1) * rows])
            hid[c] = h
            if k < ROUNDS - 1:
                hh[k, c, 1 : height + 1] = h.astype(BF16).reshape(height, width, chans)
        if k < ROUNDS - 1:
            span = pl.ds(start, n)
            return [
                push(side, hh.at[k, span, line_src[side]], hh.at[k, span, line_dst[side]])
                for side in (UP, DOWN)
            ]
        return []

    def gather(members, start, pick):
        chosen = [start + m for m, member in enumerate(members) if pick(*member)]
        total = None
        for c in chosen:
            term = times(c) * hid[c]
            total = term if total is None else total + term
        return total

    hid_edges = {}
    for k in range(ROUNDS):
        parcels = []
        for n, group in enumerate(groups):
            way, j, start, members = group
            if k == 0:
                for handle in mot_edges[n]:
                    arrive(handle)
            hid_edges[n] = recur(k, group)
            if way is not None:
                tosend = gather(members, start, lambda i, t: True).astype(BF16)
                msend[k, way, j] = dot(tosend, wmsg_s[chans : 2 * chans]).astype(BF16)
                parcels.append(push(way, msend.at[k, way, j], mrecv.at[k, way, j]))
        everything = [(c, m) for g in groups for c, m in enumerate(g[3], g[2])]
        for i in range(fd):
            first_sum = None
            second_sum = jnp.zeros((rows, chans), F32)
            for c, (s, t) in everything:
                if s == i:
                    term = times(c) * hid[c]
                    first_sum = term if first_sum is None else first_sum + term
                if t == fd + i:
                    second_sum = second_sum + times(c) * hid[c]
            pieces = jnp.concatenate([first_sum.astype(BF16), second_sum.astype(BF16)], axis=1)
            mown[i] = dot(pieces, wmsg_s[...])

        def ahead(n):
            _, _, start, members = groups[n]
            for handle in hid_edges[n]:
                arrive(handle)
            for m in range(len(members)):
                c = start + m
                hw[c] = dot(hh[k, c].reshape(tall, chans), wzr_s[0:chans])

        if k < ROUNDS - 1:
            for n in range(len(groups) - 1):
                ahead(n)
        for handle in parcels:
            arrive(handle)
        for i in range(fd):
            total = mown[i] + mrecv[k, LEFT, i].astype(F32) + mrecv[k, RIGHT, i].astype(F32)
            ubuf[k, i, 2 : height + 2] = (
                jnp.maximum(total, 0.0).astype(BF16).reshape(height, width, chans)
            )
        reach = 2 if k < ROUNDS - 1 else 1
        u_src = {UP: pl.ds(2, reach), DOWN: pl.ds(height + 2 - reach, reach)}
        u_dst = {UP: pl.ds(height + 2, reach), DOWN: pl.ds(2 - reach, reach)}
        u_edges = [
            push(side, ubuf.at[k, :, u_src[side]], ubuf.at[k, :, u_dst[side]])
            for side in (UP, DOWN)
        ]
        if k < ROUNDS - 1:
            ahead(len(groups) - 1)
        for handle in u_edges:
            arrive(handle)
        lines = height + 2 * (reach - 1)
        for i in range(fd):
            taps = [
                ubuf[k, i, 2 - reach + t : 2 - reach + t + lines].reshape(lines * width, chans)
                for t in range(3)
            ]
            moved = shifted_sum(dot(jnp.concatenate(taps, axis=1), wres_s[...]))
            old = st[k, i, 2 - reach : 2 - reach + lines] if k < ROUNDS - 1 else st[k, i, 1 : height + 1]
            new = (old.reshape(lines * width, chans).astype(F32) + moved).astype(BF16)
            new = new.reshape(lines, width, chans)
            if k == ROUNDS - 1:
                out_ref[i] = new
            else:
                st[k + 1, i] = new
        if k < ROUNDS - 1:
            for way, edge in ((UP, r == 0), (DOWN, r == nr - 1)):
                @pl.when(edge)
                def _(way=way):
                    st[k + 1, :, line_dst[back[way]]] = jnp.zeros((fd, width, chans), BF16)

    for handle in sent:
        @pl.when(both(has[handle[1]], handle[4]))
        def _(handle=handle):
            rcopy(handle).wait_send()


def local(nf, nr, fmap, context, pairs, w_corr, w_zr, w_q, w_msg, w_res):
    fd, height, width, chans = fmap.shape
    rows = height * width
    tall = rows + 2 * width
    win = 3 * fd
    groups, combos = plan(fd)
    tiles = -(-SPAN // (LANES // width))
    copies = 2 * fd + 2 + 2 + 4 * fd + 2 * len(groups) * ROUNDS + ROUNDS * (2 * fd + 2)
    hbm = pl.BlockSpec(memory_space=pl.ANY)
    return pl.pallas_call(
        functools.partial(kernel, nf, nr),
        out_shape=jax.ShapeDtypeStruct(fmap.shape, BF16),
        in_specs=[pl.BlockSpec(memory_space=pltpu.SMEM)] + [hbm] * 7,
        out_specs=pl.BlockSpec(memory_space=pltpu.VMEM),
        scratch_shapes=[
            pltpu.VMEM((height, fd, width, chans), BF16),
            pltpu.VMEM((win, 2 * RADIUS + height + 1, width, chans), BF16),
            pltpu.VMEM((ROUNDS, fd, height + 2, width, chans), BF16),
            pltpu.VMEM((combos, height + 2, width, chans), BF16),
            pltpu.VMEM((combos, rows, chans), F32),
            pltpu.VMEM((ROUNDS - 1, combos, height + 2, width, chans), BF16),
            pltpu.VMEM((fd, tall, chans), F32),
            pltpu.VMEM((fd, tall, 2 * chans), F32),
            pltpu.VMEM((combos, tall, 2 * chans), F32),
            pltpu.VMEM((combos, height + 2, width, 2 * chans), BF16),
            pltpu.VMEM((combos, rows, chans), F32),
            pltpu.VMEM((fd, rows, chans), F32),
            pltpu.VMEM((fd, rows, chans), F32),
            pltpu.VMEM((ROUNDS, 2, fd, rows, chans), BF16),
            pltpu.VMEM((ROUNDS, 2, fd, rows, chans), BF16),
            pltpu.VMEM((ROUNDS, fd, height + 4, width, chans), BF16),
            pltpu.VMEM((fd, rows, chans), F32),
            pltpu.VMEM(w_corr.shape, BF16),
            pltpu.VMEM((tiles * LANES, chans), BF16),
            pltpu.VMEM(w_zr.shape, BF16),
            pltpu.VMEM((6 * chans, 3 * chans), BF16),
            pltpu.VMEM((3 * chans, 3 * chans), BF16),
            pltpu.VMEM((2 * chans, chans), BF16),
            pltpu.SMEM((combos,), jnp.int32),
            pltpu.SemaphoreType.DMA((copies,)),
            pltpu.SemaphoreType.DMA((copies,)),
            pltpu.SemaphoreType.DMA((fd + 23,)),
        ],
        compiler_params=pltpu.CompilerParams(collective_id=0, has_side_effects=True),
    )(pairs.T, fmap, context, w_corr, w_zr, w_q, w_msg, w_res)


def solution(mesh):
    placed = (P("frames", "rows", None, None), P("frames", "rows", None, None)) + (P(),) * 6
    return jax.shard_map(
        functools.partial(local, mesh.shape["frames"], mesh.shape["rows"]),
        mesh=mesh,
        in_specs=placed,
        out_specs=P("frames", "rows", None, None),
        check_vma=False,
    )
```

time: 56.6 us -> 35.8 us (0.63)
  Pallas kernels: 53.5 us -> 34 us
  local copies, waits for them, and re-layouts: 2.91 us -> 1.54 us
    pallas_call x1, Pallas kernels: 53.5 us -> 34 us  [local(): pl.pallas_call(functools.partial(kernel, nf, nr), out_shape=jax.ShapeDtyp...]
    unnamed x2 -> x1, local copies, waits for them, and re-layouts: 2.91 us -> 1.54 us
where the time goes in v1:
time: 35.8 us; the launch traced here: 35.6 us
  Pallas kernels  34 us (95%)
  local copies, waits for them, and re-layouts  1.54 us (4%)
    pallas_call x1, Pallas kernels, local(): pl.pallas_call(functools.partial(kernel, nf, nr), out_shape=jax.ShapeDtyp...  34 us
    unnamed x1, local copies, waits for them, and re-layouts  1.54 us

profile of v1, /device:TPU:9, one launch (start us, length us, event | category | flops | bytes accessed | tf_op | source)
XLA Modules:
  0.0 35.6 jit_solution(6537757430285524322)
XLA Ops:
  0.0 34.0 %shard_map.82 = bf16[2,3,64,128]{3,2,1,0:T(8,128)(2,1)} custom-call(s32[3,32]{1,0:T(4,128)} %bitcast.1, bf16[2,3,64,128]{3,2,1,0:T(8,128)(2,1)} %fmap_ref.1, bf16[2,3,64,128]{3,2,1,0:T(8,128)(2,1)} %ctx_ref.1, bf16[49,128]{1,0:T(8,128)(2,1)} %wcorr_ref.1, bf16[256,256]{1,0:T(8,128)(2,1)} %wzr_ref.1, bf16[9,256,128]{2,1,0:T(8,128)(2,1)} %wq_ref.1, ...), custom_call_target="tpu_custom_call" | custom-call | tf_op jit(solution)/shard_map/pallas_call | solution.py:436
  34.0 1.5 %copy.10 = bf16[2,3,64,128]{3,2,1,0:T(8,128)(2,1)} copy(bf16[2,3,64,128]{3,2,1,0:T(8,128)(2,1)} %shard_map.82) | data formatting | bytes 196608

commit v2 on v1

--- a/solution.py
+++ b/solution.py
@@ -14,7 +14,7 @@
 MESH = pl.DeviceIdType.MESH
 F32 = jnp.float32
 BF16 = jnp.bfloat16
-LEFT, RIGHT, UP, DOWN = range(4)
+FAR, NEAR, UP, DOWN = range(4)
 
 
 def dot(a, b):
@@ -28,7 +28,7 @@
 def plan(fd):
     groups = []
     for j in range(fd):
-        for way, seat in ((LEFT, j), (RIGHT, 2 * fd + j)):
+        for way, seat in ((FAR, j), (NEAR, 2 * fd + j)):
             groups.append((way, j, [(i, seat) for i in range(fd)]))
     groups.append((None, 0, [(i, fd + j) for j in range(fd) for i in range(fd) if i != j]))
     start = 0
@@ -45,7 +45,7 @@
     out_ref,
     fsrc, fwin, st, mot, hid, hh, th, hw0, hw, qbuf, zbuf, asum, bsum,
     msend, mrecv, ubuf, mown,
-    wcorr_s, wsel, wzr_s, wq_s, wres_s, wmsg_s, tbl,
+    pairs_s, wcorr_s, wsel, wzr_s, wq_s, wres_s, wmsg_s, tbl,
     ssem, rsem, lsem,
 ):
     f = lax.axis_index("frames")
@@ -55,9 +55,14 @@
     rows = height * width
     tall = (height + 2) * width
     groups, total_combos = plan(fd)
-    has = {LEFT: f > 0, RIGHT: f < nf - 1, UP: r > 0, DOWN: r < nr - 1}
-    dev = {LEFT: (f - 1, r), RIGHT: (f + 1, r), UP: (f, r - 1), DOWN: (f, r + 1)}
-    back = {LEFT: RIGHT, RIGHT: LEFT, UP: DOWN, DOWN: UP}
+    step = 1 - 2 * lax.rem(f, 2)
+    near, far = f + step, f - step
+    has = {
+        FAR: jnp.logical_and(far >= 0, far < nf), NEAR: jnp.logical_and(near >= 0, near < nf),
+        UP: r > 0, DOWN: r < nr - 1,
+    }
+    dev = {FAR: (far, r), NEAR: (near, r), UP: (f, r - 1), DOWN: (f, r + 1)}
+    back = {FAR: FAR, NEAR: NEAR, UP: DOWN, DOWN: UP}
     sent = []
 
     def both(cond, gate):
@@ -87,11 +92,11 @@
 
     own_rows = pl.ds(RADIUS, height)
     middle = pl.ds(fd, fd)
-    seat = {RIGHT: 0, LEFT: 2 * fd}
+    seat = {FAR: 0, NEAR: 2 * fd}
 
     barrier = pltpu.get_barrier_semaphore()
     count = 0
-    for way in (LEFT, RIGHT, UP, DOWN):
+    for way in (FAR, NEAR, UP, DOWN):
         count = count + has[way].astype(jnp.int32)
 
         @pl.when(has[way])
@@ -108,6 +113,7 @@
 
     own_f = [load(fmap_ref.at[i], fsrc.at[:, i]) for i in range(fd)]
     own_c = load(ctx_ref, st.at[0, :, pl.ds(1, height)])
+    listed = load(pairs_ref, pairs_s)
     corr_w = load(wcorr_ref, wcorr_s)
     gate_w = load(wzr_ref, wzr_s)
     late = []
@@ -137,17 +143,15 @@
     feats = {}
     edge_src = {UP: pl.ds(RADIUS, RADIUS), DOWN: pl.ds(height, RADIUS)}
     edge_dst = {UP: pl.ds(RADIUS + height, RADIUS), DOWN: pl.ds(0, RADIUS)}
-    own_edges = []
+    own_edges = [
+        push(way, fwin.at[middle, edge_src[way]], fwin.at[middle, edge_dst[way]])
+        for way in (UP, DOWN)
+    ]
     for j in range(fd):
-        for way in (RIGHT, LEFT):
+        for way in (FAR, NEAR):
             feats[way, j] = push(
                 way, fwin.at[fd + j, own_rows], fwin.at[seat[way] + j, own_rows]
             )
-        if j == 0:
-            own_edges = [
-                push(way, fwin.at[middle, edge_src[way]], fwin.at[middle, edge_dst[way]])
-                for way in (UP, DOWN)
-            ]
     line_src = {UP: 1, DOWN: height}
     line_dst = {UP: height + 1, DOWN: 0}
     own_c.wait()
@@ -170,25 +174,28 @@
             first = 0 if way == UP else height + 2
             ubuf[:, :, first : first + 2] = jnp.zeros((ROUNDS, fd, 2, width, chans), BF16)
 
-    for way, edge in ((RIGHT, f == 0), (LEFT, f == nf - 1)):
-        @pl.when(edge)
+    for way in (FAR, NEAR):
+        @pl.when(jnp.logical_not(has[way]))
         def _(way=way):
             fwin[seat[way] : seat[way] + fd] = jnp.zeros((fd,) + fwin.shape[1:], BF16)
             for k in range(ROUNDS):
                 mrecv[k, way] = jnp.zeros((fd, rows, chans), BF16)
 
     window = 3 * fd
-    base_s = f * fd
-    base_t = (f - 1) * fd
+    bases = [base * fd for base in (far, f, near)]
     codes = [i * window + j for _, _, _, members in groups for i, j in members]
 
     def tally(p, counts):
-        i = pairs_ref[0, p] - base_s
-        j = pairs_ref[1, p] - base_t
+        i = pairs_s[0, p] - bases[1]
         own = jnp.logical_and(i >= 0, i < fd)
-        code = jnp.where(own, i * window + j, -1)
+        code = jnp.int32(-1)
+        for n, base in enumerate(bases):
+            j = pairs_s[1, p] - base
+            here = jnp.logical_and(own, jnp.logical_and(j >= 0, j < fd))
+            code = jnp.where(here, i * window + n * fd + j, code)
         return tuple(v + (code == c).astype(jnp.int32) for v, c in zip(counts, codes))
 
+    listed.wait()
     counts = lax.fori_loop(0, npair, tally, (jnp.int32(0),) * total_combos)
     for c in range(total_combos):
         tbl[c] = counts[c]
@@ -251,12 +258,10 @@
             for side in (UP, DOWN)
         ]
 
-    for handle in own_edges:
-        arrive(handle)
-    mot_edges = {len(groups) - 1: correlate(groups[-1])}
     relays = {}
-    for j in range(fd):
-        for way in (RIGHT, LEFT):
+
+    def relay(j):
+        for way in (FAR, NEAR):
             arrive(feats[way, j])
             spot = seat[way] + j
             relays[spot] = [
@@ -266,6 +271,13 @@
                 )
                 for side in (UP, DOWN)
             ]
+
+    relay(0)
+    for handle in own_edges:
+        arrive(handle)
+    mot_edges = {len(groups) - 1: correlate(groups[-1])}
+    for j in range(1, fd):
+        relay(j)
     for handle in ctx_edges:
         arrive(handle)
     gate_w.wait()
@@ -273,10 +285,16 @@
         first = jnp.tanh(st[0, i].reshape(tall, chans).astype(F32))
         th[i] = first
         hw0[i] = dot(first.astype(BF16), wzr_s[0:chans])
-    for n, group in enumerate(groups[:-1]):
-        for handle in relays[group[3][0][1]]:
+
+    def compare(n):
+        for handle in relays[groups[n][3][0][1]]:
             arrive(handle)
-        mot_edges[n] = correlate(group)
+        mot_edges[n] = correlate(groups[n])
+
+    remote = len(groups) - 1
+    early = min(4, remote)
+    for n in range(early):
+        compare(n)
     for copy in late:
         copy.wait()
 
@@ -345,17 +363,19 @@
 
     hid_edges = {}
     for k in range(ROUNDS):
-        parcels = []
+        parcels = {}
         for n, group in enumerate(groups):
             way, j, start, members = group
             if k == 0:
+                if 0 < n <= remote - early:
+                    compare(n + early - 1)
                 for handle in mot_edges[n]:
                     arrive(handle)
             hid_edges[n] = recur(k, group)
             if way is not None:
                 tosend = gather(members, start, lambda i, t: True).astype(BF16)
                 msend[k, way, j] = dot(tosend, wmsg_s[chans : 2 * chans]).astype(BF16)
-                parcels.append(push(way, msend.at[k, way, j], mrecv.at[k, way, j]))
+                parcels[way, j] = push(way, msend.at[k, way, j], mrecv.at[k, way, j])
         everything = [(c, m) for g in groups for c, m in enumerate(g[3], g[2])]
         for i in range(fd):
             first_sum = None
@@ -380,34 +400,35 @@
         if k < ROUNDS - 1:
             for n in range(len(groups) - 1):
                 ahead(n)
-        for handle in parcels:
-            arrive(handle)
+        reach = 2 if k < ROUNDS - 1 else 1
+        u_src = {UP: pl.ds(2, reach), DOWN: pl.ds(height + 2 - reach, reach)}
+        u_dst = {UP: pl.ds(height + 2, reach), DOWN: pl.ds(2 - reach, reach)}
+        u_edges = []
         for i in range(fd):
-            total = mown[i] + mrecv[k, LEFT, i].astype(F32) + mrecv[k, RIGHT, i].astype(F32)
+            for way in (FAR, NEAR):
+                arrive(parcels[way, i])
+            total = mown[i] + mrecv[k, FAR, i].astype(F32) + mrecv[k, NEAR, i].astype(F32)
             ubuf[k, i, 2 : height + 2] = (
                 jnp.maximum(total, 0.0).astype(BF16).reshape(height, width, chans)
             )
-        reach = 2 if k < ROUNDS - 1 else 1
-        u_src = {UP: pl.ds(2, reach), DOWN: pl.ds(height + 2 - reach, reach)}
-        u_dst = {UP: pl.ds(height + 2, reach), DOWN: pl.ds(2 - reach, reach)}
-        u_edges = [
-            push(side, ubuf.at[k, :, u_src[side]], ubuf.at[k, :, u_dst[side]])
-            for side in (UP, DOWN)
-        ]
+            u_edges.append([
+                push(side, ubuf.at[k, i, u_src[side]], ubuf.at[k, i, u_dst[side]])
+                for side in (UP, DOWN)
+            ])
         if k < ROUNDS - 1:
             ahead(len(groups) - 1)
-        for handle in u_edges:
-            arrive(handle)
         lines = height + 2 * (reach - 1)
         for i in range(fd):
+            for handle in u_edges[i]:
+                arrive(handle)
             taps = [
                 ubuf[k, i, 2 - reach + t : 2 - reach + t + lines].reshape(lines * width, chans)
                 for t in range(3)
             ]
             moved = shifted_sum(dot(jnp.concatenate(taps, axis=1), wres_s[...]))
-            old = st[k, i, 2 - reach : 2 - reach + lines] if k < ROUNDS - 1 else st[k, i, 1 : height + 1]
-            new = (old.reshape(lines * width, chans).astype(F32) + moved).astype(BF16)
-            new = new.reshape(lines, width, chans)
+            first = 2 - reach if k < ROUNDS - 1 else 1
+            old = st[k, i, first : first + lines].reshape(lines * width, chans)
+            new = (old.astype(F32) + moved).astype(BF16).reshape(lines, width, chans)
             if k == ROUNDS - 1:
                 out_ref[i] = new
             else:
@@ -431,12 +452,12 @@
     win = 3 * fd
     groups, combos = plan(fd)
     tiles = -(-SPAN // (LANES // width))
-    copies = 2 * fd + 2 + 2 + 4 * fd + 2 * len(groups) * ROUNDS + ROUNDS * (2 * fd + 2)
+    copies = 2 * fd + 2 + 2 + 4 * fd + 2 * len(groups) * ROUNDS + ROUNDS * 4 * fd
     hbm = pl.BlockSpec(memory_space=pl.ANY)
     return pl.pallas_call(
         functools.partial(kernel, nf, nr),
-        out_shape=jax.ShapeDtypeStruct(fmap.shape, BF16),
-        in_specs=[pl.BlockSpec(memory_space=pltpu.SMEM)] + [hbm] * 7,
+        out_shape=pltpu.VMEM(fmap.shape, BF16),
+        in_specs=[hbm] * 8,
         out_specs=pl.BlockSpec(memory_space=pltpu.VMEM),
         scratch_shapes=[
             pltpu.VMEM((height, fd, width, chans), BF16),
@@ -456,6 +477,7 @@
             pltpu.VMEM((ROUNDS, 2, fd, rows, chans), BF16),
             pltpu.VMEM((ROUNDS, fd, height + 4, width, chans), BF16),
             pltpu.VMEM((fd, rows, chans), F32),
+            pltpu.SMEM((3, pairs.shape[0]), jnp.int32),
             pltpu.VMEM(w_corr.shape, BF16),
             pltpu.VMEM((tiles * LANES, chans), BF16),
             pltpu.VMEM(w_zr.shape, BF16),
@@ -465,7 +487,7 @@
             pltpu.SMEM((combos,), jnp.int32),
             pltpu.SemaphoreType.DMA((copies,)),
             pltpu.SemaphoreType.DMA((copies,)),
-            pltpu.SemaphoreType.DMA((fd + 23,)),
+            pltpu.SemaphoreType.DMA((fd + 24,)),
         ],
         compiler_params=pltpu.CompilerParams(collective_id=0, has_side_effects=True),
     )(pairs.T, fmap, context, w_corr, w_zr, w_q, w_msg, w_res)

time: 35.8 us -> 33.1 us (0.925)
  Pallas kernels: 34 us -> 32.1 us
  local copies, waits for them, and re-layouts: 1.54 us -> 0.64 us
    pallas_call x1, Pallas kernels: 34 us -> 32.1 us  [local(): pl.pallas_call(functools.partial(kernel, nf, nr), out_shape=pltpu.VMEM(fm...]
    unnamed x1, local copies, waits for them, and re-layouts: 1.54 us -> 0.64 us
where the time goes in v2:
time: 33.1 us; the launch traced here: 32.8 us
  Pallas kernels  32.1 us (97%)
  local copies, waits for them, and re-layouts  0.64 us (2%)
    pallas_call x1, Pallas kernels, local(): pl.pallas_call(functools.partial(kernel, nf, nr), out_shape=pltpu.VMEM(fm...  32.1 us

profile of v2, /device:TPU:9, one launch (start us, length us, event | category | flops | bytes accessed | tf_op | source)
XLA Modules:
  0.0 32.8 jit_solution(3804443846161065972)
XLA Ops:
  0.0 32.1 %shard_map.82 = bf16[2,3,64,128]{3,2,1,0:T(8,128)(2,1)S(1)} custom-call(s32[3,32]{1,0:T(4,128)} %bitcast.1, bf16[2,3,64,128]{3,2,1,0:T(8,128)(2,1)} %fmap_ref.1, bf16[2,3,64,128]{3,2,1,0:T(8,128)(2,1)} %ctx_ref.1, bf16[49,128]{1,0:T(8,128)(2,1)} %wcorr_ref.1, bf16[256,256]{1,0:T(8,128)(2,1)} %wzr_ref.1, bf16[9,256,128]{2,1,0:T(8,128)(2,1)} %wq_ref.1, ...), custom_call_target="tpu_custom_call" | custom-call | tf_op jit(solution)/shard_map/pallas_call | solution.py:457
  32.1 0.6 %copy.10 = bf16[2,3,64,128]{3,2,1,0:T(8,128)(2,1)} copy(bf16[2,3,64,128]{3,2,1,0:T(8,128)(2,1)S(1)} %shard_map.82) | data formatting | bytes 196608

commit v3 on v2

--- a/solution.py
+++ b/solution.py
@@ -1,4 +1,5 @@
 import functools
+import math
 
 import jax
 import jax.numpy as jnp
@@ -9,6 +10,7 @@
 
 RADIUS = 3
 ROUNDS = 2
+LATE = True
 LANES = 128
 SPAN = 2 * RADIUS + 1
 MESH = pl.DeviceIdType.MESH
@@ -43,9 +45,9 @@
     nf, nr,
     pairs_ref, fmap_ref, ctx_ref, wcorr_ref, wzr_ref, wq_ref, wmsg_ref, wres_ref,
     out_ref,
-    fsrc, fwin, st, mot, hid, hh, th, hw0, hw, qbuf, zbuf, asum, bsum,
-    msend, mrecv, ubuf, mown,
-    pairs_s, wcorr_s, wsel, wzr_s, wq_s, wres_s, wmsg_s, tbl,
+    fsrc, fwin, st, mot, hid, hh, th, hw0, hw, qbuf, zbuf,
+    msend, mrecv, ubuf, mown, town,
+    bulk, pairs_s, wcorr_s, wsel, wzr_s, wq_s, wres_s, wmsg_s, tbl,
     ssem, rsem, lsem,
 ):
     f = lax.axis_index("frames")
@@ -63,32 +65,58 @@
     }
     dev = {FAR: (far, r), NEAR: (near, r), UP: (f, r - 1), DOWN: (f, r + 1)}
     back = {FAR: FAR, NEAR: NEAR, UP: DOWN, DOWN: UP}
-    sent = []
+    sent = {}
+    landed = []
 
     def both(cond, gate):
         return cond if gate is None else jnp.logical_and(cond, gate)
 
-    def rcopy(handle):
-        i, way, src, dst, _ = handle
+    def rcopy(way, src, dst, send_sem, recv_sem):
         return pltpu.make_async_remote_copy(
-            src_ref=src, dst_ref=dst, send_sem=ssem.at[i], recv_sem=rsem.at[i],
+            src_ref=src, dst_ref=dst, send_sem=send_sem, recv_sem=recv_sem,
             device_id=dev[way], device_id_type=MESH,
         )
 
-    def push(way, src, dst, gate=None):
-        handle = (len(sent), way, src, dst, gate)
-        sent.append(handle)
-
-        @pl.when(both(has[way], gate))
-        def _():
-            rcopy(handle).start()
-
-        return handle
+    def lines_of(ref):
+        return math.prod(ref.shape) // (width * chans)
+
+    kinds = [(way, None) for way in (FAR, NEAR, UP, DOWN)]
+    kinds += [(side, way) for side in (UP, DOWN) for way in (FAR, NEAR)]
+
+    def push(copies, gate=None):
+        spot = len(landed)
+        landed.append(None)
+        for way, src, dst in copies:
+            kind = kinds.index((way, gate))
+            sent[kind] = sent.get(kind, 0) + lines_of(src)
+
+            @pl.when(both(has[way], None if gate is None else has[gate]))
+            def _(way=way, src=src, dst=dst, kind=kind):
+                rcopy(way, src, dst, ssem.at[kind], rsem.at[spot]).start()
+
+        return spot, [way for way, _, _ in copies], lines_of(copies[0][1]), gate
+
+    def await_lines(way, spot, lines):
+        part = bulk.at[pl.ds(0, lines)]
+        rcopy(way, part, part, ssem.at[0], rsem.at[spot]).wait_recv()
 
     def arrive(handle):
-        @pl.when(both(has[back[handle[1]]], handle[4]))
-        def _():
-            rcopy(handle).wait_recv()
+        spot, ways, lines, gate = handle
+        gate = None if gate is None else has[gate]
+        if len(ways) == 1:
+            @pl.when(both(has[back[ways[0]]], gate))
+            def _():
+                await_lines(ways[0], spot, lines)
+        else:
+            here, there = (has[back[way]] for way in ways)
+
+            @pl.when(both(jnp.logical_and(here, there), gate))
+            def _():
+                await_lines(ways[0], spot, 2 * lines)
+
+            @pl.when(both(jnp.not_equal(here, there), gate))
+            def _():
+                await_lines(ways[0], spot, lines)
 
     own_rows = pl.ds(RADIUS, height)
     middle = pl.ds(fd, fd)
@@ -103,28 +131,35 @@
         def _(way=way):
             pl.semaphore_signal(barrier, inc=1, device_id=dev[way], device_id_type=MESH)
 
-    loads = []
-
-    def load(src, dst):
-        copy = pltpu.make_async_copy(src, dst, lsem.at[len(loads)])
-        loads.append(copy)
-        copy.start()
-        return copy
-
-    own_f = [load(fmap_ref.at[i], fsrc.at[:, i]) for i in range(fd)]
-    own_c = load(ctx_ref, st.at[0, :, pl.ds(1, height)])
-    listed = load(pairs_ref, pairs_s)
-    corr_w = load(wcorr_ref, wcorr_s)
-    gate_w = load(wzr_ref, wzr_s)
-    late = []
-    for k in range(3):
-        for j in range(3):
-            lanes = pl.ds(j * chans, chans)
-            late.append(load(wq_ref.at[3 * k + j], wq_s.at[pl.ds(2 * k * chans, 2 * chans), lanes]))
-            late.append(load(wres_ref.at[3 * k + j], wres_s.at[pl.ds(k * chans, chans), lanes]))
-    for k in range(2):
-        lanes = pl.ds(k * chans, chans)
-        late.append(load(wmsg_ref.at[:, lanes], wmsg_s.at[lanes]))
+    class Load:
+        def __init__(self, n, whole, copies):
+            self.n, self.whole = n, whole
+            for src, dst in copies:
+                pltpu.make_async_copy(src, dst, lsem.at[n]).start()
+
+        def wait(self):
+            pltpu.make_async_copy(self.whole, self.whole, lsem.at[self.n]).wait()
+
+    def lanes(j):
+        return pl.ds(j * chans, chans)
+
+    taps = [(k, j) for k in range(3) for j in range(3)]
+    own_f = Load(0, fsrc, [(fmap_ref.at[i], fsrc.at[:, i]) for i in range(fd)])
+    own_c = pltpu.make_async_copy(ctx_ref, st.at[0, :, pl.ds(1, height)], lsem.at[1])
+    own_c.start()
+    listed = Load(2, pairs_s, [(pairs_ref, pairs_s)])
+    corr_w = Load(3, wcorr_s, [(wcorr_ref, wcorr_s)])
+    gate_w = Load(4, wzr_s, [(wzr_ref, wzr_s)])
+    late = [
+        Load(5, wq_s, [
+            (wq_ref.at[3 * k + j], wq_s.at[pl.ds(2 * k * chans, 2 * chans), lanes(j)])
+            for k, j in taps
+        ]),
+        Load(6, wres_s, [
+            (wres_ref.at[3 * k + j], wres_s.at[lanes(k), lanes(j)]) for k, j in taps
+        ]),
+        Load(7, wmsg_s, [(wmsg_ref.at[:, lanes(k)], wmsg_s.at[lanes(k)]) for k in range(2)]),
+    ]
 
     flip = jnp.where(
         lax.broadcasted_iota(jnp.int32, (width, width), 0)
@@ -133,8 +168,7 @@
         1.0,
         0.0,
     ).astype(BF16)
-    for copy in own_f:
-        copy.wait()
+    own_f.wait()
     for i in range(fd):
         for y in range(height):
             fwin[fd + i, RADIUS + y] = dot(flip, fsrc[y, i]).astype(BF16)
@@ -143,21 +177,27 @@
     feats = {}
     edge_src = {UP: pl.ds(RADIUS, RADIUS), DOWN: pl.ds(height, RADIUS)}
     edge_dst = {UP: pl.ds(RADIUS + height, RADIUS), DOWN: pl.ds(0, RADIUS)}
-    own_edges = [
-        push(way, fwin.at[middle, edge_src[way]], fwin.at[middle, edge_dst[way]])
+    own_edges = push([
+        (way, fwin.at[middle, edge_src[way]], fwin.at[middle, edge_dst[way]])
         for way in (UP, DOWN)
-    ]
-    for j in range(fd):
+    ])
+
+    def offer(j):
         for way in (FAR, NEAR):
-            feats[way, j] = push(
-                way, fwin.at[fd + j, own_rows], fwin.at[seat[way] + j, own_rows]
-            )
+            feats[way, j] = push([
+                (way, fwin.at[fd + j, own_rows], fwin.at[seat[way] + j, own_rows])
+            ])
+
+    offer(0)
     line_src = {UP: 1, DOWN: height}
     line_dst = {UP: height + 1, DOWN: 0}
     own_c.wait()
-    ctx_edges = [
-        push(way, st.at[0, :, line_src[way]], st.at[0, :, line_dst[way]]) for way in (UP, DOWN)
-    ]
+    ctx_edges = push([
+        (way, st.at[0, :, line_src[way]], st.at[0, :, line_dst[way]]) for way in (UP, DOWN)
+    ])
+    if not LATE:
+        for j in range(1, fd):
+            offer(j)
 
     fwin[:, 2 * RADIUS + height] = jnp.zeros((fwin.shape[0],) + fwin.shape[2:], BF16)
     for way, edge in ((UP, r == 0), (DOWN, r == nr - 1)):
@@ -253,33 +293,34 @@
         n = len(members)
         mot[start : start + n, 1 : height + 1] = moved.reshape(n, height, width, chans)
         span = pl.ds(start, n)
-        return [
-            push(side, mot.at[span, line_src[side]], mot.at[span, line_dst[side]])
+        return push([
+            (side, mot.at[span, line_src[side]], mot.at[span, line_dst[side]])
             for side in (UP, DOWN)
-        ]
+        ])
 
     relays = {}
+    if LATE:
+        for j in range(1, fd):
+            offer(j)
 
     def relay(j):
         for way in (FAR, NEAR):
             arrive(feats[way, j])
             spot = seat[way] + j
-            relays[spot] = [
-                push(
-                    side, fwin.at[spot, edge_src[side]], fwin.at[spot, edge_dst[side]],
-                    gate=has[back[way]],
-                )
-                for side in (UP, DOWN)
-            ]
+            relays[spot] = push(
+                [
+                    (side, fwin.at[spot, edge_src[side]], fwin.at[spot, edge_dst[side]])
+                    for side in (UP, DOWN)
+                ],
+                gate=way,
+            )
 
     relay(0)
-    for handle in own_edges:
-        arrive(handle)
+    arrive(own_edges)
     mot_edges = {len(groups) - 1: correlate(groups[-1])}
     for j in range(1, fd):
         relay(j)
-    for handle in ctx_edges:
-        arrive(handle)
+    arrive(ctx_edges)
     gate_w.wait()
     for i in range(fd):
         first = jnp.tanh(st[0, i].reshape(tall, chans).astype(F32))
@@ -287,8 +328,7 @@
         hw0[i] = dot(first.astype(BF16), wzr_s[0:chans])
 
     def compare(n):
-        for handle in relays[groups[n][3][0][1]]:
-            arrive(handle)
+        arrive(relays[groups[n][3][0][1]])
         mot_edges[n] = correlate(groups[n])
 
     remote = len(groups) - 1
@@ -310,29 +350,35 @@
             + jnp.where(line_no < width - 1, after, 0.0)
         )
 
+    gated = set()
+
+    def gate(k, c, i):
+        gated.add((k, c))
+        state = st[k, i].reshape(tall, chans).astype(F32)
+        xin = (mot[c].reshape(tall, chans).astype(F32) + state).astype(BF16)
+        known = hw0[i] if k == 0 else hw[c]
+        gates = dot(xin, wzr_s[chans : 2 * chans]) + known
+        zbuf[c] = jax.nn.sigmoid(gates[width : width + rows, 0:chans])
+        reset = jax.nn.sigmoid(gates[:, chans : 2 * chans])
+        if k == 0:
+            h = th[i]
+        else:
+            h = jnp.concatenate(
+                [
+                    hh[k - 1, c, 0].astype(F32), hid[c],
+                    hh[k - 1, c, height + 1].astype(F32),
+                ],
+                axis=0,
+            )
+        qbuf[c, :, :, 0:chans] = (reset * h).astype(BF16).reshape(height + 2, width, chans)
+        qbuf[c, :, :, chans : 2 * chans] = xin.reshape(height + 2, width, chans)
+
     def recur(k, group):
         _, _, start, members = group
         n = len(members)
         for m, (i, _) in enumerate(members):
-            c = start + m
-            state = st[k, i].reshape(tall, chans).astype(F32)
-            xin = (mot[c].reshape(tall, chans).astype(F32) + state).astype(BF16)
-            known = hw0[i] if k == 0 else hw[c]
-            gates = dot(xin, wzr_s[chans : 2 * chans]) + known
-            zbuf[c] = jax.nn.sigmoid(gates[width : width + rows, 0:chans])
-            reset = jax.nn.sigmoid(gates[:, chans : 2 * chans])
-            if k == 0:
-                h = th[i]
-            else:
-                h = jnp.concatenate(
-                    [
-                        hh[k - 1, c, 0].astype(F32), hid[c],
-                        hh[k - 1, c, height + 1].astype(F32),
-                    ],
-                    axis=0,
-                )
-            qbuf[c, :, :, 0:chans] = (reset * h).astype(BF16).reshape(height + 2, width, chans)
-            qbuf[c, :, :, chans : 2 * chans] = xin.reshape(height + 2, width, chans)
+            if (k, start + m) not in gated:
+                gate(k, start + m, i)
         taps = [
             qbuf[start : start + n, t : t + height].reshape(n * rows, 2 * chans) for t in range(3)
         ]
@@ -347,16 +393,15 @@
                 hh[k, c, 1 : height + 1] = h.astype(BF16).reshape(height, width, chans)
         if k < ROUNDS - 1:
             span = pl.ds(start, n)
-            return [
-                push(side, hh.at[k, span, line_src[side]], hh.at[k, span, line_dst[side]])
+            return push([
+                (side, hh.at[k, span, line_src[side]], hh.at[k, span, line_dst[side]])
                 for side in (UP, DOWN)
-            ]
-        return []
-
-    def gather(members, start, pick):
-        chosen = [start + m for m, member in enumerate(members) if pick(*member)]
+            ])
+        return None
+
+    def gather(members, start):
         total = None
-        for c in chosen:
+        for c in range(start, start + len(members)):
             term = times(c) * hid[c]
             total = term if total is None else total + term
         return total
@@ -369,13 +414,13 @@
             if k == 0:
                 if 0 < n <= remote - early:
                     compare(n + early - 1)
-                for handle in mot_edges[n]:
-                    arrive(handle)
+                arrive(mot_edges[n])
             hid_edges[n] = recur(k, group)
             if way is not None:
-                tosend = gather(members, start, lambda i, t: True).astype(BF16)
-                msend[k, way, j] = dot(tosend, wmsg_s[chans : 2 * chans]).astype(BF16)
-                parcels[way, j] = push(way, msend.at[k, way, j], mrecv.at[k, way, j])
+                msend[k, way, j] = gather(members, start).astype(BF16)
+                parcels[way, j] = push([
+                    (way, msend.at[k, way, j], mrecv.at[k, way, j])
+                ])
         everything = [(c, m) for g in groups for c, m in enumerate(g[3], g[2])]
         for i in range(fd):
             first_sum = None
@@ -386,63 +431,105 @@
                     first_sum = term if first_sum is None else first_sum + term
                 if t == fd + i:
                     second_sum = second_sum + times(c) * hid[c]
-            pieces = jnp.concatenate([first_sum.astype(BF16), second_sum.astype(BF16)], axis=1)
-            mown[i] = dot(pieces, wmsg_s[...])
+            mown[i] = dot(first_sum.astype(BF16), wmsg_s[0:chans])
+            town[i] = second_sum
 
         def ahead(n):
             _, _, start, members = groups[n]
-            for handle in hid_edges[n]:
-                arrive(handle)
+            arrive(hid_edges[n])
             for m in range(len(members)):
                 c = start + m
                 hw[c] = dot(hh[k, c].reshape(tall, chans), wzr_s[0:chans])
 
-        if k < ROUNDS - 1:
-            for n in range(len(groups) - 1):
-                ahead(n)
         reach = 2 if k < ROUNDS - 1 else 1
+        lines = height + 2 * (reach - 1)
         u_src = {UP: pl.ds(2, reach), DOWN: pl.ds(height + 2 - reach, reach)}
         u_dst = {UP: pl.ds(height + 2, reach), DOWN: pl.ds(2 - reach, reach)}
-        u_edges = []
-        for i in range(fd):
+        u_edges = {}
+
+        def update(i):
             for way in (FAR, NEAR):
                 arrive(parcels[way, i])
-            total = mown[i] + mrecv[k, FAR, i].astype(F32) + mrecv[k, NEAR, i].astype(F32)
+            arrived = mrecv[k, FAR, i].astype(F32) + mrecv[k, NEAR, i].astype(F32)
+            second = (town[i] + arrived).astype(BF16)
+            total = mown[i] + dot(second, wmsg_s[chans : 2 * chans])
             ubuf[k, i, 2 : height + 2] = (
                 jnp.maximum(total, 0.0).astype(BF16).reshape(height, width, chans)
             )
-            u_edges.append([
-                push(side, ubuf.at[k, i, u_src[side]], ubuf.at[k, i, u_dst[side]])
+            u_edges[i] = push([
+                (side, ubuf.at[k, i, u_src[side]], ubuf.at[k, i, u_dst[side]])
                 for side in (UP, DOWN)
             ])
-        if k < ROUNDS - 1:
-            ahead(len(groups) - 1)
-        lines = height + 2 * (reach - 1)
-        for i in range(fd):
-            for handle in u_edges[i]:
-                arrive(handle)
+
+        def inner(i):
+            own = ubuf[k, i, 2 : height + 2].reshape(rows, chans)
+            acc = dot(own, wres_s[chans : 2 * chans])
+            blank = jnp.zeros((width, 3 * chans), F32)
+            if height > 1:
+                above = dot(own[: rows - width], wres_s[0:chans])
+                below = dot(own[width:], wres_s[2 * chans : 3 * chans])
+                acc = acc + jnp.concatenate([blank, above], axis=0)
+                acc = acc + jnp.concatenate([below, blank], axis=0)
+            old = st[k, i, 1 : height + 1].reshape(rows, chans)
+            mown[i] = old.astype(F32) + shifted_sum(acc)
+
+        def outer(i):
+            arrive(u_edges[i])
+            above = shifted_sum(dot(ubuf[k, i, 1], wres_s[0:chans]))
+            below = shifted_sum(dot(ubuf[k, i, height + 2], wres_s[2 * chans : 3 * chans]))
+            for y in range(height):
+                total = mown[i, y * width : (y + 1) * width]
+                if y == 0:
+                    total = total + above
+                if y == height - 1:
+                    total = total + below
+                out_ref[i, y] = total.astype(BF16)
+
+        def residual(i):
+            arrive(u_edges[i])
             taps = [
                 ubuf[k, i, 2 - reach + t : 2 - reach + t + lines].reshape(lines * width, chans)
                 for t in range(3)
             ]
             moved = shifted_sum(dot(jnp.concatenate(taps, axis=1), wres_s[...]))
-            first = 2 - reach if k < ROUNDS - 1 else 1
-            old = st[k, i, first : first + lines].reshape(lines * width, chans)
+            old = st[k, i].reshape(lines * width, chans)
             new = (old.astype(F32) + moved).astype(BF16).reshape(lines, width, chans)
-            if k == ROUNDS - 1:
-                out_ref[i] = new
-            else:
-                st[k + 1, i] = new
-        if k < ROUNDS - 1:
+            st[k + 1, i] = new
             for way, edge in ((UP, r == 0), (DOWN, r == nr - 1)):
                 @pl.when(edge)
                 def _(way=way):
-                    st[k + 1, :, line_dst[back[way]]] = jnp.zeros((fd, width, chans), BF16)
-
-    for handle in sent:
-        @pl.when(both(has[handle[1]], handle[4]))
-        def _(handle=handle):
-            rcopy(handle).wait_send()
+                    st[k + 1, i, line_dst[back[way]]] = jnp.zeros((width, chans), BF16)
+
+        fill = list(range(len(groups))) if k < ROUNDS - 1 else []
+        for i in range(fd):
+            update(i)
+            for n in fill[: 2]:
+                ahead(n)
+            fill = fill[2:]
+        if k == ROUNDS - 1:
+            for i in range(fd):
+                inner(i)
+            for i in range(fd):
+                outer(i)
+        for i in range(fd if k < ROUNDS - 1 else 0):
+            residual(i)
+            if k < ROUNDS - 1:
+                for n in fill:
+                    ahead(n)
+                fill = []
+                if i < fd - 1:
+                    for _, _, start, members in groups:
+                        for m, (source, _) in enumerate(members):
+                            if source == i:
+                                gate(k + 1, start + m, source)
+
+    for kind, lines in sorted(sent.items()):
+        way, gate = kinds[kind]
+
+        @pl.when(both(has[way], None if gate is None else has[gate]))
+        def _(way=way, kind=kind, lines=lines):
+            part = bulk.at[pl.ds(0, lines)]
+            rcopy(way, part, part, ssem.at[kind], rsem.at[0]).wait_send()
 
 
 def local(nf, nr, fmap, context, pairs, w_corr, w_zr, w_q, w_msg, w_res):
@@ -452,7 +539,7 @@
     win = 3 * fd
     groups, combos = plan(fd)
     tiles = -(-SPAN // (LANES // width))
-    copies = 2 * fd + 2 + 2 + 4 * fd + 2 * len(groups) * ROUNDS + ROUNDS * 4 * fd
+    copies = 4 * fd + 2 + len(groups) * ROUNDS + ROUNDS * 3 * fd
     hbm = pl.BlockSpec(memory_space=pl.ANY)
     return pl.pallas_call(
         functools.partial(kernel, nf, nr),
@@ -471,12 +558,12 @@
             pltpu.VMEM((combos, tall, 2 * chans), F32),
             pltpu.VMEM((combos, height + 2, width, 2 * chans), BF16),
             pltpu.VMEM((combos, rows, chans), F32),
-            pltpu.VMEM((fd, rows, chans), F32),
-            pltpu.VMEM((fd, rows, chans), F32),
             pltpu.VMEM((ROUNDS, 2, fd, rows, chans), BF16),
             pltpu.VMEM((ROUNDS, 2, fd, rows, chans), BF16),
             pltpu.VMEM((ROUNDS, fd, height + 4, width, chans), BF16),
             pltpu.VMEM((fd, rows, chans), F32),
+            pltpu.VMEM((fd, rows, chans), F32),
+            pltpu.VMEM((ROUNDS * (combos + 2 * fd) + 4 * fd, width, chans), BF16),
             pltpu.SMEM((3, pairs.shape[0]), jnp.int32),
             pltpu.VMEM(w_corr.shape, BF16),
             pltpu.VMEM((tiles * LANES, chans), BF16),
@@ -485,9 +572,9 @@
             pltpu.VMEM((3 * chans, 3 * chans), BF16),
             pltpu.VMEM((2 * chans, chans), BF16),
             pltpu.SMEM((combos,), jnp.int32),
+            pltpu.SemaphoreType.DMA((8,)),
             pltpu.SemaphoreType.DMA((copies,)),
-            pltpu.SemaphoreType.DMA((copies,)),
-            pltpu.SemaphoreType.DMA((fd + 24,)),
+            pltpu.SemaphoreType.DMA((8,)),
         ],
         compiler_params=pltpu.CompilerParams(collective_id=0, has_side_effects=True),
     )(pairs.T, fmap, context, w_corr, w_zr, w_q, w_msg, w_res)

time: 33.1 us -> 31.9 us (0.964)
  Pallas kernels: 32.1 us -> 31.1 us
    pallas_call x1, Pallas kernels: 32.1 us -> 31.1 us  [local(): pl.pallas_call(functools.partial(kernel, nf, nr), out_shape=pltpu.VMEM(fm...]
where the time goes in v3:
time: 31.9 us; the launch traced here: 31.8 us
  Pallas kernels  31.1 us (97%)
  local copies, waits for them, and re-layouts  0.64 us (2%)
    pallas_call x1, Pallas kernels, local(): pl.pallas_call(functools.partial(kernel, nf, nr), out_shape=pltpu.VMEM(fm...  31.1 us
    unnamed x1, local copies, waits for them, and re-layouts  0.64 us

profile of v3, /device:TPU:9, one launch (start us, length us, event | category | flops | bytes accessed | tf_op | source)
XLA Modules:
  0.0 31.8 jit_solution(1578562083841973868)
XLA Ops:
  0.0 31.1 %shard_map.82 = bf16[2,3,64,128]{3,2,1,0:T(8,128)(2,1)S(1)} custom-call(s32[3,32]{1,0:T(4,128)} %bitcast.1, bf16[2,3,64,128]{3,2,1,0:T(8,128)(2,1)} %fmap_ref.1, bf16[2,3,64,128]{3,2,1,0:T(8,128)(2,1)} %ctx_ref.1, bf16[49,128]{1,0:T(8,128)(2,1)} %wcorr_ref.1, bf16[256,256]{1,0:T(8,128)(2,1)} %wzr_ref.1, bf16[9,256,128]{2,1,0:T(8,128)(2,1)} %wq_ref.1, ...), custom_call_target="tpu_custom_call" | custom-call | tf_op jit(solution)/shard_map/pallas_call | solution.py:544
  31.1 0.6 %copy.10 = bf16[2,3,64,128]{3,2,1,0:T(8,128)(2,1)} copy(bf16[2,3,64,128]{3,2,1,0:T(8,128)(2,1)S(1)} %shard_map.82) | data formatting | bytes 196608

commit v4 on v3

--- a/solution.py
+++ b/solution.py
@@ -10,7 +10,6 @@
 
 RADIUS = 3
 ROUNDS = 2
-LATE = True
 LANES = 128
 SPAN = 2 * RADIUS + 1
 MESH = pl.DeviceIdType.MESH
@@ -177,11 +176,6 @@
     feats = {}
     edge_src = {UP: pl.ds(RADIUS, RADIUS), DOWN: pl.ds(height, RADIUS)}
     edge_dst = {UP: pl.ds(RADIUS + height, RADIUS), DOWN: pl.ds(0, RADIUS)}
-    own_edges = push([
-        (way, fwin.at[middle, edge_src[way]], fwin.at[middle, edge_dst[way]])
-        for way in (UP, DOWN)
-    ])
-
     def offer(j):
         for way in (FAR, NEAR):
             feats[way, j] = push([
@@ -189,15 +183,19 @@
             ])
 
     offer(0)
+    own_edges = push([
+        (way, fwin.at[middle, edge_src[way]], fwin.at[middle, edge_dst[way]])
+        for way in (UP, DOWN)
+    ])
+
     line_src = {UP: 1, DOWN: height}
     line_dst = {UP: height + 1, DOWN: 0}
     own_c.wait()
     ctx_edges = push([
         (way, st.at[0, :, line_src[way]], st.at[0, :, line_dst[way]]) for way in (UP, DOWN)
     ])
-    if not LATE:
-        for j in range(1, fd):
-            offer(j)
+    for j in range(1, fd):
+        offer(j)
 
     fwin[:, 2 * RADIUS + height] = jnp.zeros((fwin.shape[0],) + fwin.shape[2:], BF16)
     for way, edge in ((UP, r == 0), (DOWN, r == nr - 1)):
@@ -275,6 +273,10 @@
         return jnp.concatenate(pieces, axis=1)
 
     def correlate(group):
+        correlate_rows(group)
+        return edge_lines(group)
+
+    def correlate_rows(group):
         way, _, start, members = group
         lines = [[] for _ in members]
         for y in range(height):
@@ -292,16 +294,15 @@
         moved = jnp.maximum(dot(corr, wsel[...]) * scale, 0.0).astype(BF16)
         n = len(members)
         mot[start : start + n, 1 : height + 1] = moved.reshape(n, height, width, chans)
-        span = pl.ds(start, n)
+
+    def edge_lines(group):
+        span = pl.ds(group[2], len(group[3]))
         return push([
             (side, mot.at[span, line_src[side]], mot.at[span, line_dst[side]])
             for side in (UP, DOWN)
         ])
 
     relays = {}
-    if LATE:
-        for j in range(1, fd):
-            offer(j)
 
     def relay(j):
         for way in (FAR, NEAR):
@@ -315,17 +316,31 @@
                 gate=way,
             )
 
+    def start_hidden(when):
+        @pl.when(when)
+        def _():
+            arrive(ctx_edges)
+            gate_w.wait()
+            for i in range(fd):
+                first = jnp.tanh(st[0, i].reshape(tall, chans).astype(F32))
+                th[i] = first
+                hw0[i] = dot(first.astype(BF16), wzr_s[0:chans])
+
+    def compare_own(when):
+        @pl.when(when)
+        def _():
+            arrive(own_edges)
+            correlate_rows(groups[-1])
+
+    even_row = lax.rem(r, 2) == 0
+    compare_own(even_row)
+    start_hidden(even_row)
     relay(0)
-    arrive(own_edges)
-    mot_edges = {len(groups) - 1: correlate(groups[-1])}
+    compare_own(jnp.logical_not(even_row))
+    mot_edges = {len(groups) - 1: edge_lines(groups[-1])}
     for j in range(1, fd):
         relay(j)
-    arrive(ctx_edges)
-    gate_w.wait()
-    for i in range(fd):
-        first = jnp.tanh(st[0, i].reshape(tall, chans).astype(F32))
-        th[i] = first
-        hw0[i] = dot(first.astype(BF16), wzr_s[0:chans])
+    start_hidden(jnp.logical_not(even_row))
 
     def compare(n):
         arrive(relays[groups[n][3][0][1]])
@@ -415,6 +430,8 @@
                 if 0 < n <= remote - early:
                     compare(n + early - 1)
                 arrive(mot_edges[n])
+            if k > 0 and n == remote:
+                last_ahead()
             hid_edges[n] = recur(k, group)
             if way is not None:
                 msend[k, way, j] = gather(members, start).astype(BF16)
@@ -434,9 +451,9 @@
             mown[i] = dot(first_sum.astype(BF16), wmsg_s[0:chans])
             town[i] = second_sum
 
-        def ahead(n):
+        def ahead(n, k=k, edges=dict(hid_edges)):
             _, _, start, members = groups[n]
-            arrive(hid_edges[n])
+            arrive(edges[n])
             for m in range(len(members)):
                 c = start + m
                 hw[c] = dot(hh[k, c].reshape(tall, chans), wzr_s[0:chans])
@@ -500,28 +517,20 @@
                 def _(way=way):
                     st[k + 1, i, line_dst[back[way]]] = jnp.zeros((width, chans), BF16)
 
-        fill = list(range(len(groups))) if k < ROUNDS - 1 else []
         for i in range(fd):
             update(i)
-            for n in fill[: 2]:
-                ahead(n)
-            fill = fill[2:]
+            if k < ROUNDS - 1:
+                for n in range(i * remote // fd, (i + 1) * remote // fd):
+                    ahead(n)
         if k == ROUNDS - 1:
             for i in range(fd):
                 inner(i)
             for i in range(fd):
                 outer(i)
-        for i in range(fd if k < ROUNDS - 1 else 0):
-            residual(i)
-            if k < ROUNDS - 1:
-                for n in fill:
-                    ahead(n)
-                fill = []
-                if i < fd - 1:
-                    for _, _, start, members in groups:
-                        for m, (source, _) in enumerate(members):
-                            if source == i:
-                                gate(k + 1, start + m, source)
+        else:
+            for i in range(fd):
+                residual(i)
+        last_ahead = functools.partial(ahead, remote)
 
     for kind, lines in sorted(sent.items()):
         way, gate = kinds[kind]

time: 31.9 us -> 31.5 us (0.987)
  Pallas kernels: 31.1 us -> 30.7 us
    pallas_call x1, Pallas kernels: 31.1 us -> 30.7 us  [local(): pl.pallas_call(functools.partial(kernel, nf, nr), out_shape=pltpu.VMEM(fm...]
where the time goes in v4:
time: 31.5 us; the launch traced here: 31.3 us
  Pallas kernels  30.7 us (97%)
  local copies, waits for them, and re-layouts  0.64 us (2%)
    pallas_call x1, Pallas kernels, local(): pl.pallas_call(functools.partial(kernel, nf, nr), out_shape=pltpu.VMEM(fm...  30.7 us
    unnamed x1, local copies, waits for them, and re-layouts  0.64 us

profile of v4, /device:TPU:9, one launch (start us, length us, event | category | flops | bytes accessed | tf_op | source)
XLA Modules:
  0.0 31.3 jit_solution(4387181276181805942)
XLA Ops:
  0.0 30.7 %shard_map.82 = bf16[2,3,64,128]{3,2,1,0:T(8,128)(2,1)S(1)} custom-call(s32[3,32]{1,0:T(4,128)} %bitcast.1, bf16[2,3,64,128]{3,2,1,0:T(8,128)(2,1)} %fmap_ref.1, bf16[2,3,64,128]{3,2,1,0:T(8,128)(2,1)} %ctx_ref.1, bf16[49,128]{1,0:T(8,128)(2,1)} %wcorr_ref.1, bf16[256,256]{1,0:T(8,128)(2,1)} %wzr_ref.1, bf16[9,256,128]{2,1,0:T(8,128)(2,1)} %wq_ref.1, ...), custom_call_target="tpu_custom_call" | custom-call | tf_op jit(solution)/shard_map/pallas_call | solution.py:553
  30.7 0.6 %copy.10 = bf16[2,3,64,128]{3,2,1,0:T(8,128)(2,1)} copy(bf16[2,3,64,128]{3,2,1,0:T(8,128)(2,1)S(1)} %shard_map.82) | data formatting | bytes 196608
